TPU v7x, 32 devices: a whole 2x2x4 slice. The times are simulated.
32 devices in a mesh: front: 2 (over y), row: 4 (over z), col: 4 (over x, core).
Axes of the slice: x: 2, y: 2, z: 4, core: 2. Of those that a mesh axis runs over, the one named last changes fastest.
Arguments:
- pivot: float32 [2, 512, 512], P('front', ('row', 'col')), may hold values from -1 to 8
- col_ut: bfloat16 [2, 4, 96, 512], P('front', 'row', None, 'col'), may hold values from -6 to 6
- col_vt: bfloat16 [2, 4, 96, 512], P('front', 'row', None, 'col'), may hold values from -0.25 to 0.25
- col_rank: int32 [2, 4], P('front', 'row'), may hold values from 32 to 96
- row_ut: bfloat16 [2, 4, 96, 512], P('front', 'col', None, 'row'), may hold values from -6 to 6
- row_vt: bfloat16 [2, 4, 96, 512], P('front', 'col', None, 'row'), may hold values from -0.625 to 0.625
- row_rank: int32 [2, 4], P('front', 'col'), may hold values from 32 to 96
- cb_ut: bfloat16 [2, 4, 4, 96, 512], P('front', 'row', 'col'), may hold values from -6 to 6
- cb_vt: bfloat16 [2, 4, 4, 96, 512], P('front', 'row', 'col'), may hold values from -0.625 to 0.625
- cb_rank: int32 [2, 4, 4], P('front', 'row', 'col'), may hold values from 32 to 96
- parent_map: int32 [2, 4], P('front'), may hold values from 0 to 7, as said below
Outputs:
- parent_tiles: bfloat16 [2, 8, 4, 512, 512], P('front', 'row', 'col')
Inputs may be any that keep to these rules, and one draw needn't show every extreme that they name: `parent_map`: for every front the entries are distinct; entry 0 is 4, and 0 and 7 both appear.
All inputs are finite; a program needn't handle non-finite values.
Results may differ from a plain program's by a relative error of at most 0.0062.
Values may be sent and summed in bfloat16 or wider, within the bound.
A program may use at most 64 MiB of HBM per device.

v0:
```python
import jax
import jax.numpy as jnp
from jax import lax
from jax.sharding import PartitionSpec as P

NS_ITERS = 2


HIGH = lax.Precision.HIGHEST


def swapped(x, axis, bit):
    return lax.ppermute(x, axis, [(i, i ^ 1 << bit) for i in range(lax.axis_size(axis))])


def ranked(factor, rank):
    levels = jnp.arange(factor.shape[-2], dtype=jnp.int32)[:, None]
    keep = levels < rank[..., None, None]
    return jnp.where(keep, factor, jnp.zeros_like(factor))


def densify(left, right):
    return jnp.einsum("ijkx,ijky->ijxy", left, right, preferred_element_type=jnp.float32).astype(
        jnp.bfloat16
    )


def selector(mapping, first, count):
    wanted = first + jnp.arange(count, dtype=jnp.int32)
    return (mapping[None, :] == wanted[:, None]).astype(jnp.bfloat16)


def fold_rows(select_rows, carry, pieces):
    results = []
    for total, piece in zip(carry, pieces):
        count = piece.shape[0]
        flat = piece.reshape(count, -1)
        moved = jnp.dot(select_rows, flat, preferred_element_type=jnp.float32).astype(jnp.bfloat16)
        results.append(moved.reshape(total.shape))
    return tuple(results)


def fold_cols(select_cols, carry, pieces):
    results = []
    for total, piece in zip(carry, pieces):
        count = piece.shape[1]
        flat = piece.reshape(piece.shape[0], count, -1)
        moved = jnp.einsum(
            "bj,ajx->abx", select_cols, flat, preferred_element_type=jnp.float32
        ).astype(jnp.bfloat16)
        results.append(moved.reshape(total.shape))
    return tuple(results)


def shards(
    pivot, col_ut, col_vt, col_rank, row_ut, row_vt, row_rank, cb_ut, cb_vt, cb_rank, parent_map
):
    whole = lax.all_gather(pivot[0], ("row", "col"), axis=0, tiled=True)
    eye = jnp.eye(whole.shape[0], dtype=jnp.float32)
    approx = eye / jnp.diagonal(whole)[None, :]
    for step in range(NS_ITERS):
        approx = jnp.dot(approx, 2.0 * eye - jnp.dot(whole, approx, precision=HIGH), precision=HIGH)
    column_left, column_right = (
        lax.all_gather(col_ut[0], "col", axis=2, tiled=True),
        lax.all_gather(col_vt[0], "col", axis=2, tiled=True),
    )
    column_left = ranked(column_left, col_rank[0])
    column_right = ranked(column_right, col_rank[0])
    lower = jnp.einsum(
        "atx,xy->aty", column_right.astype(jnp.float32), approx, precision=HIGH
    ).astype(jnp.bfloat16)
    upper_left, upper_right = (
        lax.all_gather(row_ut[0], "row", axis=2, tiled=True),
        lax.all_gather(row_vt[0], "row", axis=2, tiled=True),
    )
    upper_left = ranked(upper_left, row_rank[0])
    upper_right = ranked(upper_right, row_rank[0])
    core = jnp.einsum(
        "iax,jbx->ijab", lower, upper_left, preferred_element_type=jnp.float32
    ).astype(jnp.bfloat16)
    update = jnp.einsum(
        "ijab,iax->ijbx", core, column_left, preferred_element_type=jnp.float32
    ).astype(jnp.bfloat16)
    block_left = ranked(cb_ut[0], cb_rank[0])
    block_right = ranked(cb_vt[0], cb_rank[0])
    rows_here = block_left.shape[0]
    cols_here = block_left.shape[1]
    left = jnp.concatenate([block_left, -update], axis=2)
    right = jnp.concatenate([block_right, upper_right[None]], axis=2)
    parent_rows = 2 * rows_here
    select_rows = selector(parent_map[0], lax.axis_index("row") * parent_rows, parent_rows)
    select_cols = selector(parent_map[0], lax.axis_index("col") * parent_rows, parent_rows)
    factor_shape = left.shape[2:]
    empty_rows = jnp.zeros((parent_rows, cols_here) + factor_shape, jnp.bfloat16)
    rows_left, rows_right = fold_rows(
        select_rows,
        (empty_rows, empty_rows),
        (
            lax.all_gather(left, "row", axis=0, tiled=True),
            lax.all_gather(right, "row", axis=0, tiled=True),
        ),
    )
    empty_cols = jnp.zeros((parent_rows, parent_rows) + factor_shape, jnp.bfloat16)
    both_left, both_right = fold_cols(
        select_cols,
        (empty_cols, empty_cols),
        (
            lax.all_gather(rows_left, "col", axis=1, tiled=True),
            lax.all_gather(rows_right, "col", axis=1, tiled=True),
        ),
    )
    placed = densify(both_left, both_right)
    side = lax.axis_index("front") % 2
    mine = lax.dynamic_slice_in_dim(placed, side * cols_here, cols_here, 1)
    other = lax.dynamic_slice_in_dim(placed, (1 - side) * cols_here, cols_here, 1)
    received = swapped(other, "front", 0)
    total = mine.astype(jnp.float32) + received.astype(jnp.float32)
    return total.astype(jnp.bfloat16)[None]


def solution(mesh):
    placed = (
        P("front", ("row", "col"), None),
        P("front", "row", None, "col"),
        P("front", "row", None, "col"),
        P("front", "row"),
        P("front", "col", None, "row"),
        P("front", "col", None, "row"),
        P("front", "col"),
        P("front", "row", "col", None, None),
        P("front", "row", "col", None, None),
        P("front", "row", "col"),
        P("front", None),
    )
    return jax.shard_map(
        shards,
        mesh=mesh,
        in_specs=placed,
        out_specs=P("front", "row", "col", None, None),
        check_vma=False,
    )
```

profile of v0, /device:TPU:0, one launch (start us, length us, event | category | flops | bytes accessed | tf_op | source)
XLA Modules:
  0.0 174.1 jit_solution(11467706569666828324)
XLA Ops:
  6.5 0.0 all-gather.13.cloned.1.call-start
  6.5 0.7 all-gather.13.cloned.1.call-update
  7.3 0.0 all-gather.11.cloned.1.call-start
  8.6 14.0 %all-gather.4 = bf16[1,1,96,512]{3,2,1,0:T(8,128)(2,1)S(1)} all-gather(bf16[1,1,96,128]{3,2,1,0:T(8,128)(2,1)} %param.16), channel_id=6, replica_groups=mesh['front'=2,'row'=4,'col'=4] {'row'}, dimensions={3}, use_global_device_ids=true | all-gather | bytes 122880 | tf_op jit(solution)/shard_map/all_gather | solution.py:74
  22.7 0.1 fusion.11
  22.7 1.0 bitcast_select_fusion.1
  23.8 0.0 copy-start.4
  23.8 19.5 %all_gather.34 = bf16[4,1,192,512]{3,2,1,0:T(8,128)(2,1)S(1)} all-gather(bf16[1,1,192,512]{3,2,1,0:T(8,128)(2,1)S(1)} %pad_maximum_fusion.1), channel_id=1, replica_groups=mesh['front'=2,'row'=4,'col'=4] {'row'}, dimensions={0}, use_global_device_ids=true | all-gather | bytes 983040 | tf_op jit(solution)/shard_map/all_gather | solution.py:100
  43.3 0.6 copy.25
  43.9 0.0 copy-start.1
  43.9 0.0 copy-start.2
  43.9 0.0 copy-start.3
  44.0 0.0 copy-done.4
  44.0 0.6 convolution_convert_fusion.2
  44.6 0.8 copy.33
  45.4 0.0 all-gather.11.cloned.1.call-update
  45.4 0.0 all-gather.9.cloned.1.call-start
  46.1 0.0 copy-done.1
  46.1 5.4 %all-gather.1 = bf16[1,1,96,512]{3,2,1,0:T(8,128)(2,1)S(1)} all-gather(bf16[1,1,96,128]{3,2,1,0:T(8,128)(2,1)S(1)} %copy-done.1), channel_id=3, replica_groups=mesh['front'=2,'row'=4,'col'=4] {'col'}, dimensions={3}, use_global_device_ids=true | all-gather | bytes 122880 | tf_op jit(solution)/shard_map/all_gather | solution.py:65
  51.5 0.0 copy-done.2
  51.5 12.2 %all-gather = bf16[1,1,96,512]{3,2,1,0:T(8,128)(2,1)S(1)} all-gather(bf16[1,1,96,128]{3,2,1,0:T(8,128)(2,1)S(1)} %copy-done.2), channel_id=2, replica_groups=mesh['front'=2,'row'=4,'col'=4] {'row'}, dimensions={3}, use_global_device_ids=true | all-gather | bytes 122880 | tf_op jit(solution)/shard_map/all_gather | solution.py:73
  63.7 0.0 copy-done.3
  63.7 6.1 %all-gather.3 = bf16[1,1,96,512]{3,2,1,0:T(8,128)(2,1)S(1)} all-gather(bf16[1,1,96,128]{3,2,1,0:T(8,128)(2,1)S(1)} %copy-done.3), channel_id=5, replica_groups=mesh['front'=2,'row'=4,'col'=4] {'col'}, dimensions={3}, use_global_device_ids=true | all-gather | bytes 122880 | tf_op jit(solution)/shard_map/all_gather | solution.py:64
  69.9 0.0 all-gather.13.cloned.1.call-done
  69.9 0.0 copy-start
  69.9 8.9 %gather_fusion = f32[512]{0:T(512)S(1)} fusion(f32[512,512]{1,0:T(8,128)} %bitcast.117, s32[512]{0:T(512)S(1)} %bitcast.116), kind=kCustom, calls=%fused_computation | custom fusion | bytes 8192 | tf_op jit(solution)/shard_map/jit(diagonal)/cond/branch_0_fun/gather | solution.py:60
  78.7 0.0 copy-done
  78.7 1.9 %select_subtract_fusion.1 = f32[512,512]{0,1:T(8,128)S(1)} fusion(f32[512]{0:T(512)S(1)} %gather_fusion, f32[1,512,512]{2,1,0:T(8,128)S(1)} %copy-done), kind=kOutput, calls=%fused_computation.12 | convolution fusion | flops 1612185600 | bytes 2099200 | tf_op jit(solution)/shard_map/dot_general | solution.py:62
  80.6 3.6 %fusion.8 = f32[512,512]{1,0:T(8,128)S(1)} fusion(f32[512,512]{0,1:T(8,128)S(1)} %select_subtract_fusion.1, f32[512]{0:T(512)S(1)} %gather_fusion), kind=kOutput, calls=%fused_computation.24 | convolution fusion | flops 1611399168 | bytes 2099200 | tf_op jit(solution)/shard_map/dot_general | solution.py:62
  84.2 3.5 %select_subtract_fusion = f32[512,512]{0,1:T(8,128)S(1)} fusion(f32[512,512]{1,0:T(8,128)S(1)} %fusion.8, f32[1,512,512]{2,1,0:T(8,128)S(1)} %copy-done), kind=kOutput, calls=%fused_computation.11 | convolution fusion | flops 1611399168 | bytes 3145728 | tf_op jit(solution)/shard_map/dot_general | solution.py:62
  87.7 1.9 %fusion.42 = f32[512,512]{1,0:T(8,128)S(1)} fusion(f32[512,512]{1,0:T(8,128)S(1)} %fusion.8, f32[512,512]{0,1:T(8,128)S(1)} %select_subtract_fusion), kind=kOutput, calls=%fused_computation.71 | convolution fusion | flops 1610612736 | bytes 3145728 | tf_op jit(solution)/shard_map/dot_general | solution.py:62
  89.6 0.5 convolution_convert_fusion.5
  90.1 0.4 fusion.5
  90.5 18.0 %all_gather.31 = bf16[4,1,192,512]{3,2,1,0:T(8,128)(2,1)S(1)} all-gather(bf16[1,1,192,512]{3,2,1,0:T(8,128)(2,1)S(1)} %pad_maximum_fusion), channel_id=1, replica_groups=mesh['front'=2,'row'=4,'col'=4] {'row'}, dimensions={0}, use_global_device_ids=true | all-gather | bytes 983040 | tf_op jit(solution)/shard_map/all_gather | solution.py:99
  108.5 0.6 copy.23
  109.1 0.6 convolution_convert_fusion.3
  109.8 0.8 copy.34
  110.6 0.0 all-gather.9.cloned.1.call-update
  110.6 0.0 all-gather.11.cloned.1.call-done
  110.6 2.9 %reshape.171 = bf16[2,4,98304]{2,0,1:T(2,128)(2,1)S(1)} reshape(bf16[2,4,192,512]{3,2,0,1:T(8,128)(2,1)} %all-gather.11.cloned.1.call-done) | data formatting | bytes 3145728 | tf_op jit(solution)/shard_map/reshape | solution.py:47
  113.6 2.2 %fusion.1 = bf16[2,2,98304]{2,1,0:T(2,128)(2,1)} fusion(bf16[2,4,98304]{2,0,1:T(2,128)(2,1)S(1)} %reshape.171, s32[4]{0:T(128)S(1)} %bitcast.128, s32[2]{0:T(128)S(1)} %iota_add_fusion), kind=kOutput, calls=%fused_computation.4 | convolution fusion | flops 3538952 | bytes 2359320 | tf_op jit(solution)/shard_map/bj,ajx->abx/dot_general | solution.py:48
  115.8 1.7 reshape.157
  117.5 12.5 %all-gather.9.cloned.1.call-done = bf16[2,4,192,512]{3,2,0,1:T(8,128)(2,1)} async-done(((bf16[2,1,192,512]{3,2,0,1:T(8,128)(2,1)}), bf16[2,4,192,512]{3,2,0,1:T(8,128)(2,1)}) %all-gather.9.cloned.1.call-update) | async-done | bytes 1572880 | tf_op jit(solution)/shard_map/all_gather | solution.py:108
  130.0 2.9 %reshape.170 = bf16[2,4,98304]{2,0,1:T(2,128)(2,1)S(1)} reshape(bf16[2,4,192,512]{3,2,0,1:T(8,128)(2,1)} %all-gather.9.cloned.1.call-done) | data formatting | bytes 3145728 | tf_op jit(solution)/shard_map/reshape | solution.py:47
  132.9 2.2 %fusion = bf16[2,2,98304]{2,1,0:T(2,128)(2,1)} fusion(bf16[2,4,98304]{2,0,1:T(2,128)(2,1)S(1)} %reshape.170, s32[4]{0:T(128)S(1)} %bitcast.129, s32[2]{0:T(128)S(1)} %iota_add_fusion), kind=kOutput, calls=%fused_computation.3 | convolution fusion | flops 3538952 | bytes 2359320 | tf_op jit(solution)/shard_map/bj,ajx->abx/dot_general | solution.py:48
  135.2 2.4 %reshape.153 = bf16[2,2,192,512]{3,2,1,0:T(8,128)(2,1)} reshape(bf16[2,2,98304]{2,1,0:T(2,128)(2,1)} %fusion) | data formatting | bytes 1572864 | tf_op jit(solution)/shard_map/reshape | solution.py:51
  137.6 1.9 %convolution_convert_fusion.4 = bf16[2,2,512,512]{3,2,1,0:T(8,128)(2,1)S(1)} fusion(bf16[2,2,192,512]{3,2,1,0:T(8,128)(2,1)} %reshape.153, bf16[2,2,192,512]{3,2,1,0:T(8,128)(2,1)S(1)} %reshape.157), kind=kOutput, calls=%fused_computation.8 | convolution fusion | flops 403701760 | bytes 3670016 | tf_op jit(solution)/shard_map/ijkx,ijky->ijxy/dot_general | solution.py:23
  139.6 0.1 constant_dynamic-slice_fusion
  139.7 1.5 collective-permute-start
  141.2 23.9 %collective-permute-done = bf16[2,1,512,512]{3,2,1,0:T(8,128)(2,1)} collective-permute-done((bf16[2,1,512,512]{3,2,1,0:T(8,128)(2,1)S(1)}, bf16[2,1,512,512]{3,2,1,0:T(8,128)(2,1)}, u32[]{:S(2)}, u32[]{:S(2)}) %collective-permute-start) | collective-permute-done | bytes 1048608 | tf_op jit(solution)/shard_map/ppermute | solution.py:13
  165.1 2.5 %fusion.7 = bf16[1,2,1,512,512]{4,3,2,1,0:T(8,128)(2,1)} fusion(bf16[2,1,512,512]{3,2,1,0:T(8,128)(2,1)} %collective-permute-done, bf16[2,2,512,512]{3,2,1,0:T(8,128)(2,1)S(1)} %convolution_convert_fusion.4, s32[]{:T(128)S(6)} %select_n.60), kind=kLoop, calls=%fused_computation.21 | loop fusion | flops 2097152 | bytes 3145732 | tf_op jit(solution)/shard_map/broadcast_in_dim | solution.py:118
  (8 shorter events, 0.1 us)
Async XLA Ops:
  6.5 63.3 %all-gather.13.cloned.1.call-start = ((), (), s32[]{:S(2)}) async-start(), calls=%async_computation.2 | async-start | bytes 1114112 | tf_op jit(solution)/shard_map/all_gather | solution.py:58
  7.3 103.4 %all-gather.11.cloned.1.call-start = ((), (), s32[]{:S(2)}) async-start(), calls=%async_computation.1 | async-start | bytes 1966080 | tf_op jit(solution)/shard_map/all_gather | solution.py:109
  23.8 20.2 %copy-start.4 = (s32[1,4]{1,0:T(1,128)S(1)}, s32[1,4]{1,0:T(1,128)}, u32[]{:S(2)}) copy-start(s32[1,4]{1,0:T(1,128)} %param.21) | copy-start | bytes 52
  43.9 2.2 %copy-start.1 = (bf16[1,1,96,128]{3,2,1,0:T(8,128)(2,1)S(1)}, bf16[1,1,96,128]{3,2,1,0:T(8,128)(2,1)}, u32[]{:S(2)}) copy-start(bf16[1,1,96,128]{3,2,1,0:T(8,128)(2,1)} %param.13) | copy-start | bytes 73732
  43.9 7.6 %copy-start.2 = (bf16[1,1,96,128]{3,2,1,0:T(8,128)(2,1)S(1)}, bf16[1,1,96,128]{3,2,1,0:T(8,128)(2,1)}, u32[]{:S(2)}) copy-start(bf16[1,1,96,128]{3,2,1,0:T(8,128)(2,1)} %param.15) | copy-start | bytes 73732
  43.9 19.8 %copy-start.3 = (bf16[1,1,96,128]{3,2,1,0:T(8,128)(2,1)S(1)}, bf16[1,1,96,128]{3,2,1,0:T(8,128)(2,1)}, u32[]{:S(2)}) copy-start(bf16[1,1,96,128]{3,2,1,0:T(8,128)(2,1)} %param.12) | copy-start | bytes 73732
  45.4 84.6 %all-gather.9.cloned.1.call-start = ((), (), s32[]{:S(2)}) async-start(), calls=%async_computation | async-start | bytes 1966080 | tf_op jit(solution)/shard_map/all_gather | solution.py:108
  69.9 8.9 %copy-start = (f32[1,512,512]{2,1,0:T(8,128)S(1)}, f32[1,512,512]{2,1,0:T(8,128)}, u32[]{:S(2)}) copy-start(f32[1,512,512]{2,1,0:T(8,128)} %all-gather.13.cloned.1.call-done) | copy-start | bytes 3145732
  139.7 25.5 %collective-permute-start = (bf16[2,1,512,512]{3,2,1,0:T(8,128)(2,1)S(1)}, bf16[2,1,512,512]{3,2,1,0:T(8,128)(2,1)}, u32[]{:S(2)}, u32[]{:S(2)}) collective-permute-start(bf16[2,1,512,512]{3,2,1,0:T(8,128)(2,1)S(1)} %constant_dynamic-slice_fusion), channel_id=1, source_target_pairs={{0,16},{16,0},{1,17},{17,1},{2,18},{18,2},{3,19},{19,3},{4,20},{20... | collective-permute-start | bytes 3145736 | tf_op jit(solution)/shard_map/ppermute | solution.py:13
Sparse Core Ops, SparseCore 0:
  9.5 41.5 all-gather.12
  52.6 19.0 all-gather.10
  110.7 19.2 all-gather.8
where the time goes:
time: 175 us; the launch traced here: 174 us
  blocking collectives  75.3 us (43%)
  waiting for transfers between devices  37.1 us (21%)
  local copies, waits for them, and re-layouts  21.8 us (12%)
  matrix products  19.4 us (11%)
  between operations  15.3 us (9%)
  other arithmetic  3.65 us (2%)
    ppermute x1, waiting for transfers between devices, swapped(): lax.ppermute(x, axis, [(i, i ^ 1 << bit) for i in range(lax.axis_size(axi...  23.9 us
    all_gather x1, blocking collectives, shards(): lax.all_gather(right, 'row', axis=0, tiled=True)  19.5 us
    all_gather x1, blocking collectives, shards(): lax.all_gather(left, 'row', axis=0, tiled=True)  18 us
    all_gather x1, blocking collectives, shards(): lax.all_gather(row_vt[0], 'row', axis=2, tiled=True)  14 us
    all_gather x1, waiting for transfers between devices, shards(): lax.all_gather(rows_left, 'col', axis=1, tiled=True)  12.5 us
    all_gather x1, blocking collectives, shards(): lax.all_gather(row_ut[0], 'row', axis=2, tiled=True)  12.2 us
    gather x1, local copies, waits for them, and re-layouts, shards(): approx = eye / jnp.diagonal(whole)[None, :]  8.85 us
    all_gather x1, blocking collectives, shards(): lax.all_gather(col_ut[0], 'col', axis=2, tiled=True)  6.14 us
  transfers between devices with their start and end apart: 4, of which 2 were waited for; matrix products, arithmetic and copies ran while one was open for 19% of the time, Pallas kernels for 0%

commit v1 on v0

v1 whole, which is shorter than its diff:
```python
import functools

import jax
import jax.numpy as jnp
from jax import lax
from jax.experimental import pallas as pl
from jax.experimental.pallas import tpu as pltpu
from jax.sharding import PartitionSpec as P

MESH = pl.DeviceIdType.MESH
F32 = jnp.float32
BF16 = jnp.bfloat16


def mm(a, b, dims):
    return lax.dot_general(a, b, (dims, ((), ())), preferred_element_type=F32)


def kernel(
    n_row,
    n_col,
    pivot,
    col_ut,
    col_vt,
    row_ut,
    row_vt,
    cb_ut,
    cb_vt,
    col_rank,
    row_rank,
    cb_rank,
    pmap,
    out,
    mbuf,
    fbuf,
    ubuf,
    vbuf,
    su,
    sv,
    yu,
    yv,
    yd,
    yr,
    zu,
    zv,
    zd,
    zr,
    rsem_p,
    ssem_p,
    rsem_c,
    ssem_c,
    rsem_s,
    ssem_s,
    rsem_y,
    ssem_y,
):
    front, r, c = lax.axis_index("front"), lax.axis_index("row"), lax.axis_index("col")
    n_x = n_col // 2
    x, core = c // 2, c % 2
    partner = 2 * x + 1 - core
    sibling = front + 1 - 2 * (front % 2)
    half = front % 2
    peers = [lax.rem(x + k, n_x) * 2 + core for k in range(1, n_x)]
    wc, wr = col_ut.shape[-1], row_ut.shape[-1]
    rank_dim, tile = cb_ut.shape[-2], cb_ut.shape[-1]
    mr = pivot.shape[1]
    has_left, has_right = r > 0, r < n_row - 1

    barrier = pltpu.get_barrier_semaphore()

    def greet(target):
        pl.semaphore_signal(barrier, inc=1, device_id=target, device_id_type=MESH)

    greet((sibling, r, c))
    greet((front, r, partner))
    for p in peers:
        greet((front, r, p))

    @pl.when(has_left)
    def _():
        greet((front, r - 1, c))

    @pl.when(has_right)
    def _():
        greet((front, r + 1, c))

    me = r * n_col + c
    rows_at = lax.broadcasted_iota(jnp.int32, (mr, tile), 0) + me * mr
    lanes_at = lax.broadcasted_iota(jnp.int32, (mr, tile), 1)
    on_diag = rows_at == lanes_at
    mine = pivot[0]
    inv = 1.0 / jnp.sum(jnp.where(on_diag, mine, 0.0), axis=1, keepdims=True)
    mbuf[me] = jnp.where(on_diag, inv, mine * inv).astype(BF16)

    def masked(value, rank):
        level = lax.broadcasted_iota(jnp.int32, value.shape, 0)
        return jnp.where(level < rank, value.astype(F32), 0.0).astype(BF16)

    fbuf[me] = jnp.concatenate(
        [
            col_ut[0, 0],
            masked(col_vt[0, 0], col_rank[0, 0]),
            masked(row_ut[0, 0], row_rank[0, 0]),
            row_vt[0, 0],
        ],
        axis=1,
    )
    ubuf[r] = masked(cb_ut[0, 0, 0], cb_rank[0, 0, 0])
    vbuf[r] = cb_vt[0, 0, 0]

    greeted = 2 + len(peers) + has_left.astype(jnp.int32) + has_right.astype(jnp.int32)
    pl.semaphore_wait(barrier, greeted)

    def copy(ref, send, recv, target):
        return pltpu.make_async_remote_copy(
            src_ref=ref, dst_ref=ref, send_sem=send, recv_sem=recv, device_id=target, device_id_type=MESH
        )

    left_dev, right_dev = (front, r - 1, c), (front, r + 1, c)
    partner_dev = (front, r, partner)
    panel = (mbuf, fbuf)

    def pcopy(t, q, cc, k, target):
        slot = q * n_col + cc
        return copy(panel[t].at[slot], ssem_p.at[t, slot, k], rsem_p.at[t, slot], target)

    def ccopy(t, q, k, target):
        return copy((ubuf, vbuf)[t].at[q], ssem_c.at[t, q, k], rsem_c.at[t, q], target)

    def z_start(make, q, came_right, came_left):
        if came_right:

            @pl.when(has_right)
            def _():
                make(2, right_dev).start()

        if came_left:

            @pl.when(has_left)
            def _():
                make(1, left_dev).start()

    def x_start(t, q):
        for k, p in enumerate(peers):
            pcopy(t, q, c, 3 + k, (front, r, p)).start()
        pcopy(t, q, c, 0, partner_dev).start()

    def hop(s):
        if s == 0:
            for t in range(2):
                z_start(lambda k, d, t=t: pcopy(t, r, c, k, d), r, True, True)
                x_start(t, r)
            for t in range(2):
                z_start(lambda k, d, t=t: ccopy(t, r, k, d), r, True, True)
            return

        def arrive(q, right):
            for t in range(2):
                pcopy(t, q, c, 0, partner_dev).wait_recv()
                z_start(lambda k, d, t=t: pcopy(t, q, c, k, d), q, right, not right)
                x_start(t, q)
            for t in range(2):
                ccopy(t, q, 0, partner_dev).wait_recv()
                z_start(lambda k, d, t=t: ccopy(t, q, k, d), q, right, not right)

        @pl.when(r - s >= 0)
        def _():
            arrive(r - s, True)

        @pl.when(r + s < n_row)
        def _():
            arrive(r + s, False)

    for s in range(n_row):
        hop(s)

    def find(wanted):
        at, found = jnp.int32(0), jnp.int32(0)
        for i in range(pmap.shape[1]):
            hit = pmap[0, i] == wanted
            at, found = jnp.where(hit, i, at), jnp.where(hit, 1, found)
        return at, found.astype(F32)

    i_at = [find(2 * r + u) for u in range(2)]
    j_own, j_sib = find(2 * c + half), find(2 * c + 1 - half)

    def kept(value, flag):
        return (value.astype(F32) * flag).astype(BF16)

    for u in range(2):
        at, found = i_at[u]
        su[c, u] = kept(ubuf[at], found)
        sv[c, u] = vbuf[at]

    stacks = (su, sv)

    def scopy(t, cc, k, target):
        return copy(stacks[t].at[cc], ssem_s.at[t, cc, k], rsem_s.at[t, cc], target)

    for t in range(2):
        for k, p in enumerate(peers):
            scopy(t, c, 1 + k, (front, r, p)).start()
        scopy(t, c, 0, partner_dev).start()

    for s in range(n_row):

        def relay(q):
            for t in range(2):
                for p in peers:
                    pcopy(t, q, p, 0, partner_dev).wait_recv()
                    pcopy(t, q, p, 0, partner_dev).start()

        @pl.when(r - s >= 0)
        def _():
            relay(r - s)

        if s > 0:

            @pl.when(r + s < n_row)
            def _():
                relay(r + s)

    others = [lax.rem(x + k, n_x) * 2 + 1 - core for k in range(n_x)]
    for q in range(n_row):
        for t in range(2):
            for p in others:
                pcopy(t, q, p, 0, partner_dev).wait_recv()

    pivots = mbuf[...].reshape(tile, tile)
    diag_blocks = []
    lane_block = 128
    for b in range(tile // lane_block):
        total = jnp.zeros((1, lane_block), F32)
        for d in range(lane_block // mr):
            dev = b * (lane_block // mr) + d
            piece = mbuf[dev, :, b * lane_block : (b + 1) * lane_block].astype(F32)
            at_r = lax.broadcasted_iota(jnp.int32, piece.shape, 0) + d * mr
            at_l = lax.broadcasted_iota(jnp.int32, piece.shape, 1)
            total = total + jnp.sum(jnp.where(at_r == at_l, piece, 0.0), axis=0, keepdims=True)
        diag_blocks.append(total)
    diag = jnp.concatenate(diag_blocks, axis=1)

    def col_piece(at, first):
        return jnp.concatenate(
            [fbuf[at * n_col + k][:, first : first + wc] for k in range(n_col)], axis=1
        )

    def row_piece(at, first):
        return jnp.concatenate(
            [fbuf[k * n_col + at][:, first : first + wr] for k in range(n_row)], axis=1
        )

    v = jnp.concatenate([col_piece(i_at[u][0], wc) for u in range(2)], axis=0)
    v32 = v.astype(F32)
    t = v
    for step in range(3):
        t32 = v32 - (mm(t, pivots, ((1,), (0,))) - t.astype(F32) * diag)
        t = t32.astype(BF16)
    lower = (t32 * diag).astype(BF16)
    col_u = [col_piece(i_at[u][0], 0) for u in range(2)]

    def updates(j):
        at, found = j
        core_ = mm(lower, row_piece(at, 2 * wc), ((1,), (1,))).astype(BF16)
        return [
            (
                mm(core_[u * rank_dim : (u + 1) * rank_dim], col_u[u], ((0,), (0,)))
                * (-found * i_at[u][1])
            ).astype(BF16)
            for u in range(2)
        ]

    ends = ((yd, zd), (yr, zr), (yu, zu), (yv, zv))

    def ycopy(t):
        return pltpu.make_async_remote_copy(
            src_ref=ends[t][0],
            dst_ref=ends[t][1],
            send_sem=ssem_y.at[t],
            recv_sem=rsem_y.at[t],
            device_id=(sibling, r, c),
            device_id_type=MESH,
        )

    yr[...] = row_piece(j_sib[0], 2 * wc + wr)
    ycopy(1).start()
    for u, value in enumerate(updates(j_sib)):
        yd[u] = value
    ycopy(0).start()

    for t in range(2):
        for p in peers:
            scopy(t, p, 0, partner_dev).wait_recv()
            scopy(t, p, 0, partner_dev).start()
    for t in range(2):
        for p in others:
            scopy(t, p, 0, partner_dev).wait_recv()
    for u in range(2):
        yu[u] = kept(su[j_sib[0], u], j_sib[1])
    ycopy(2).start()
    for u in range(2):
        yv[u] = sv[j_sib[0], u]
    ycopy(3).start()

    own = updates(j_own)
    own_r = row_piece(j_own[0], 2 * wc + wr)
    lefts = [
        jnp.concatenate([kept(su[j_own[0], u], j_own[1]), own[u]], axis=0) for u in range(2)
    ]
    rights = [jnp.concatenate([sv[j_own[0], u], own_r], axis=0) for u in range(2)]
    for t in range(4):
        ycopy(t).wait_recv()
    for u in range(2):
        left = jnp.concatenate([lefts[u], zu[u], zd[u]], axis=0)
        right = jnp.concatenate([rights[u], zv[u], zr[...]], axis=0)
        out[0, u, 0] = mm(left, right, ((0,), (0,))).astype(BF16)

    for t in range(4):
        ycopy(t).wait_send()
    for t in range(2):
        for k, p in enumerate(peers):
            scopy(t, c, 1 + k, partner_dev).wait_send()
            scopy(t, p, 0, partner_dev).wait_send()
        scopy(t, c, 0, partner_dev).wait_send()
        for q in range(n_row):
            for k, p in enumerate(peers):
                pcopy(t, q, c, 3 + k, partner_dev).wait_send()
                pcopy(t, q, p, 0, partner_dev).wait_send()
            pcopy(t, q, c, 0, partner_dev).wait_send()

            @pl.when((q <= r) & has_right)
            def _():
                pcopy(t, q, c, 2, partner_dev).wait_send()
                ccopy(t, q, 2, partner_dev).wait_send()

            @pl.when((q >= r) & has_left)
            def _():
                pcopy(t, q, c, 1, partner_dev).wait_send()
                ccopy(t, q, 1, partner_dev).wait_send()


def shards(
    n_row,
    n_col,
    pivot,
    col_ut,
    col_vt,
    col_rank,
    row_ut,
    row_vt,
    row_rank,
    cb_ut,
    cb_vt,
    cb_rank,
    parent_map,
):
    n_x = n_col // 2
    mr = pivot.shape[1]
    rank_dim, tile = cb_ut.shape[-2], cb_ut.shape[-1]
    width = 2 * col_ut.shape[-1] + 2 * row_ut.shape[-1]
    vmem = pl.BlockSpec(memory_space=pltpu.VMEM)
    smem = pl.BlockSpec(memory_space=pltpu.SMEM)
    pair = (2, rank_dim, tile)
    dma = pltpu.SemaphoreType.DMA
    return pl.pallas_call(
        functools.partial(kernel, n_row, n_col),
        out_shape=jax.ShapeDtypeStruct((1, 2, 1, tile, tile), BF16),
        in_specs=[vmem] * 7 + [smem] * 4,
        out_specs=vmem,
        scratch_shapes=[
            pltpu.VMEM((n_row * n_col, mr, tile), BF16),
            pltpu.VMEM((n_row * n_col, rank_dim, width), BF16),
            pltpu.VMEM((n_row, rank_dim, tile), BF16),
            pltpu.VMEM((n_row, rank_dim, tile), BF16),
            pltpu.VMEM((n_col,) + pair, BF16),
            pltpu.VMEM((n_col,) + pair, BF16),
            pltpu.VMEM(pair, BF16),
            pltpu.VMEM(pair, BF16),
            pltpu.VMEM(pair, BF16),
            pltpu.VMEM(pair[1:], BF16),
            pltpu.VMEM(pair, BF16),
            pltpu.VMEM(pair, BF16),
            pltpu.VMEM(pair, BF16),
            pltpu.VMEM(pair[1:], BF16),
            dma((2, n_row * n_col)),
            dma((2, n_row * n_col, 2 + n_x)),
            dma((2, n_row)),
            dma((2, n_row, 3)),
            dma((2, n_col)),
            dma((2, n_col, n_x)),
            dma((4,)),
            dma((4,)),
        ],
        compiler_params=pltpu.CompilerParams(
            collective_id=0, has_side_effects=True, vmem_limit_bytes=40 * 1024 * 1024
        ),
    )(
        pivot,
        col_ut,
        col_vt,
        row_ut,
        row_vt,
        cb_ut,
        cb_vt,
        col_rank,
        row_rank,
        cb_rank,
        parent_map,
    )


def solution(mesh):
    placed = (
        P("front", ("row", "col"), None),
        P("front", "row", None, "col"),
        P("front", "row", None, "col"),
        P("front", "row"),
        P("front", "col", None, "row"),
        P("front", "col", None, "row"),
        P("front", "col"),
        P("front", "row", "col", None, None),
        P("front", "row", "col", None, None),
        P("front", "row", "col"),
        P("front", None),
    )
    return jax.shard_map(
        functools.partial(shards, mesh.shape["row"], mesh.shape["col"]),
        mesh=mesh,
        in_specs=placed,
        out_specs=P("front", "row", "col", None, None),
        check_vma=False,
    )
```

time: 175 us -> 59.7 us (0.34)
  blocking collectives: 75.3 us -> 0 us
  Pallas kernels: 0 us -> 50.6 us
  waiting for transfers between devices: 37.1 us -> 0 us
  matrix products: 19.4 us -> 0 us
  local copies, waits for them, and re-layouts: 21.8 us -> 6.54 us
  between operations: 15.3 us -> 1.99 us
  other arithmetic: 3.65 us -> 0 us
    all_gather x6 -> x0, blocking collectives: 75.3 us -> none  [the longest x1 19.5 us: shards(): lax.all_gather(right, 'row', axis=0, tiled=True)]
    pallas_call x0 -> x1, Pallas kernels: none -> 50.6 us  [shards(): pl.pallas_call(functools.partial(kernel, n_row, n_col), out_shape=jax.Sha...]
    ppermute x1 -> x0, waiting for transfers between devices: 23.9 us -> none  [swapped(): lax.ppermute(x, axis, [(i, i ^ 1 << bit) for i in range(lax.axis_size(axi...]
    dot_general x11 -> x0, matrix products: 19.4 us -> none  [the longest x2 5.44 us: shards(): jnp.dot(approx, 2.0 * eye - jnp.dot(whole, approx, precision=HIGH), preci...]
    all_gather x3 -> x0, waiting for transfers between devices: 12.5 us -> none  [the longest x1 12.5 us: shards(): lax.all_gather(rows_left, 'col', axis=1, tiled=True)]
    reshape x4 -> x0, local copies, waits for them, and re-layouts: 10 us -> none  [the longest x2 5.87 us: fold_cols(): flat = piece.reshape(piece.shape[0], count, -1)]
    gather x1 -> x0, local copies, waits for them, and re-layouts: 8.85 us -> none  [shards(): approx = eye / jnp.diagonal(whole)[None, :]]
    unnamed x14 -> x17, local copies, waits for them, and re-layouts: 2.83 us -> 6.54 us
  transfers between devices with their start and end apart: 4 -> 0, of which waited for: 2 -> 0; matrix products, arithmetic and copies ran while one was open for 19% -> 0% of each run, Pallas kernels for 0% -> 0%
where the time goes in v1:
time: 59.7 us; the launch traced here: 59.1 us
  Pallas kernels  50.6 us (85%)
  local copies, waits for them, and re-layouts  6.54 us (11%)
  between operations  1.99 us (3%)
    pallas_call x1, Pallas kernels, shards(): pl.pallas_call(functools.partial(kernel, n_row, n_col), out_shape=jax.Sha...  50.6 us
    unnamed x17, local copies, waits for them, and re-layouts  6.54 us

profile of v1, /device:TPU:0, one launch (start us, length us, event | category | flops | bytes accessed | tf_op | source)
XLA Modules:
  0.0 59.1 jit_solution(6080775613485857359)
XLA Ops:
  1.3 0.0 copy-start.7
  2.0 0.0 copy-done.7
  2.0 0.0 copy-start
  2.0 0.9 %copy-done = bf16[1,1,1,96,512]{4,3,2,1,0:T(8,128)(2,1)S(1)} copy-done((bf16[1,1,1,96,512]{4,3,2,1,0:T(8,128)(2,1)S(1)}, bf16[1,1,1,96,512]{4,3,2,1,0:T(8,128)(2,1)}, u32[]{:S(2)}) %copy-start) | copy-done | bytes 98328
  2.9 0.0 copy-start.1
  2.9 0.9 %copy-done.1 = bf16[1,1,1,96,512]{4,3,2,1,0:T(8,128)(2,1)S(1)} copy-done((bf16[1,1,1,96,512]{4,3,2,1,0:T(8,128)(2,1)S(1)}, bf16[1,1,1,96,512]{4,3,2,1,0:T(8,128)(2,1)}, u32[]{:S(2)}) %copy-start.1) | copy-done | bytes 98328
  3.8 0.0 copy-start.2
  3.8 0.8 %copy-done.2 = f32[1,32,512]{2,1,0:T(8,128)S(1)} copy-done((f32[1,32,512]{2,1,0:T(8,128)S(1)}, f32[1,32,512]{2,1,0:T(8,128)}, u32[]{:S(2)}) %copy-start.2) | copy-done | bytes 65560
  4.6 0.0 copy-start.3
  4.6 0.7 %copy-done.3 = bf16[1,1,96,128]{3,2,1,0:T(8,128)(2,1)S(1)} copy-done((bf16[1,1,96,128]{3,2,1,0:T(8,128)(2,1)S(1)}, bf16[1,1,96,128]{3,2,1,0:T(8,128)(2,1)}, u32[]{:S(2)}) %copy-start.3) | copy-done | bytes 24600
  5.3 0.0 copy-start.4
  5.3 0.7 %copy-done.4 = bf16[1,1,96,128]{3,2,1,0:T(8,128)(2,1)S(1)} copy-done((bf16[1,1,96,128]{3,2,1,0:T(8,128)(2,1)S(1)}, bf16[1,1,96,128]{3,2,1,0:T(8,128)(2,1)}, u32[]{:S(2)}) %copy-start.4) | copy-done | bytes 24600
  6.1 0.0 copy-start.5
  6.1 0.7 %copy-done.5 = bf16[1,1,96,128]{3,2,1,0:T(8,128)(2,1)S(1)} copy-done((bf16[1,1,96,128]{3,2,1,0:T(8,128)(2,1)S(1)}, bf16[1,1,96,128]{3,2,1,0:T(8,128)(2,1)}, u32[]{:S(2)}) %copy-start.5) | copy-done | bytes 24600
  6.8 0.0 copy-start.6
  6.8 0.7 %copy-done.6 = bf16[1,1,96,128]{3,2,1,0:T(8,128)(2,1)S(1)} copy-done((bf16[1,1,96,128]{3,2,1,0:T(8,128)(2,1)S(1)}, bf16[1,1,96,128]{3,2,1,0:T(8,128)(2,1)}, u32[]{:S(2)}) %copy-start.6) | copy-done | bytes 24600
  7.6 50.6 %shard_map.109 = bf16[1,2,1,512,512]{4,3,2,1,0:T(8,128)(2,1)S(1)} custom-call(f32[1,32,512]{2,1,0:T(8,128)S(1)} %copy-done.2, bf16[1,1,96,128]{3,2,1,0:T(8,128)(2,1)S(1)} %copy-done.3, bf16[1,1,96,128]{3,2,1,0:T(8,128)(2,1)S(1)} %copy-done.4, bf16[1,1,96,128]{3,2,1,0:T(8,128)(2,1)S(1)} %copy-done.5, bf16[1,1,96,128]{3,2,1,0:T(8,128)(2,1)S(1)} %copy-done.6, ...), custom_call_target="tpu_custom_call" | custom-call | tf_op jit(solution)/shard_map/pallas_call | solution.py:365
  58.1 1.0 %copy.16 = bf16[1,2,1,512,512]{4,3,2,1,0:T(8,128)(2,1)} copy(bf16[1,2,1,512,512]{4,3,2,1,0:T(8,128)(2,1)S(1)} %shard_map.109) | data formatting | bytes 2097152
Async XLA Ops:
  1.3 0.7 %copy-start.7 = (s32[1,4]{1,0:T(1,128)S(1)}, s32[1,4]{1,0:T(1,128)}, u32[]{:S(2)}) copy-start(s32[1,4]{1,0:T(1,128)} %pmap.1) | copy-start | bytes 52
  2.0 0.9 %copy-start = (bf16[1,1,1,96,512]{4,3,2,1,0:T(8,128)(2,1)S(1)}, bf16[1,1,1,96,512]{4,3,2,1,0:T(8,128)(2,1)}, u32[]{:S(2)}) copy-start(bf16[1,1,1,96,512]{4,3,2,1,0:T(8,128)(2,1)} %cb_ut.1) | copy-start | bytes 294916
  2.9 0.9 %copy-start.1 = (bf16[1,1,1,96,512]{4,3,2,1,0:T(8,128)(2,1)S(1)}, bf16[1,1,1,96,512]{4,3,2,1,0:T(8,128)(2,1)}, u32[]{:S(2)}) copy-start(bf16[1,1,1,96,512]{4,3,2,1,0:T(8,128)(2,1)} %cb_vt.1) | copy-start | bytes 294916
  3.8 0.8 %copy-start.2 = (f32[1,32,512]{2,1,0:T(8,128)S(1)}, f32[1,32,512]{2,1,0:T(8,128)}, u32[]{:S(2)}) copy-start(f32[1,32,512]{2,1,0:T(8,128)} %pivot.1) | copy-start | bytes 196612
  4.6 0.7 %copy-start.3 = (bf16[1,1,96,128]{3,2,1,0:T(8,128)(2,1)S(1)}, bf16[1,1,96,128]{3,2,1,0:T(8,128)(2,1)}, u32[]{:S(2)}) copy-start(bf16[1,1,96,128]{3,2,1,0:T(8,128)(2,1)} %col_ut.1) | copy-start | bytes 73732
  5.3 0.7 %copy-start.4 = (bf16[1,1,96,128]{3,2,1,0:T(8,128)(2,1)S(1)}, bf16[1,1,96,128]{3,2,1,0:T(8,128)(2,1)}, u32[]{:S(2)}) copy-start(bf16[1,1,96,128]{3,2,1,0:T(8,128)(2,1)} %col_vt.1) | copy-start | bytes 73732
  6.1 0.7 %copy-start.5 = (bf16[1,1,96,128]{3,2,1,0:T(8,128)(2,1)S(1)}, bf16[1,1,96,128]{3,2,1,0:T(8,128)(2,1)}, u32[]{:S(2)}) copy-start(bf16[1,1,96,128]{3,2,1,0:T(8,128)(2,1)} %row_ut.1) | copy-start | bytes 73732
  6.8 0.7 %copy-start.6 = (bf16[1,1,96,128]{3,2,1,0:T(8,128)(2,1)S(1)}, bf16[1,1,96,128]{3,2,1,0:T(8,128)(2,1)}, u32[]{:S(2)}) copy-start(bf16[1,1,96,128]{3,2,1,0:T(8,128)(2,1)} %row_vt.1) | copy-start | bytes 73732

commit v2 on v1

v2 whole, which is shorter than its diff:
```python
import functools

import jax
import jax.numpy as jnp
from jax import lax
from jax.experimental import pallas as pl
from jax.experimental.pallas import tpu as pltpu
from jax.sharding import PartitionSpec as P

MESH = pl.DeviceIdType.MESH
F32 = jnp.float32
BF16 = jnp.bfloat16


def mm(a, b, dims):
    return lax.dot_general(a, b, (dims, ((), ())), preferred_element_type=F32)


def kernel(
    n_row,
    n_col,
    pivot_hbm,
    col_ut_hbm,
    col_vt_hbm,
    row_ut_hbm,
    row_vt_hbm,
    cb_ut_hbm,
    cb_vt_hbm,
    col_rank_hbm,
    row_rank_hbm,
    cb_rank_hbm,
    pmap_hbm,
    out,
    pivot,
    col_ut,
    col_vt,
    row_ut,
    row_vt,
    col_rank,
    row_rank,
    cb_rank,
    pmap,
    mbuf,
    fbuf,
    c0,
    c1,
    c2,
    c3,
    s0,
    s1,
    s2,
    s3,
    ybuf,
    yd,
    yr,
    zbuf,
    zd,
    zr,
    in_sem,
    rsem_p,
    ssem_p,
    rsem_c,
    ssem_c,
    rsem_s,
    ssem_s,
    rsem_y,
    ssem_y,
):
    cbuf, sbuf = (c0, c1, c2, c3), (s0, s1, s2, s3)
    front, r, c = lax.axis_index("front"), lax.axis_index("row"), lax.axis_index("col")
    n_x = n_col // 2
    x, core = c // 2, c % 2
    partner = 2 * x + 1 - core
    sibling = front + 1 - 2 * (front % 2)
    half = front % 2
    peers = [lax.rem(x + k, n_x) * 2 + core for k in range(1, n_x)]
    wc, wr = col_ut.shape[-1], row_ut.shape[-1]
    rank_dim, tile = cb_ut_hbm.shape[-2], cb_ut_hbm.shape[-1]
    wide = tile // 2
    mr = pivot.shape[1]
    has_left, has_right = r > 0, r < n_row - 1

    def chunk_src(k):
        return (cb_ut_hbm, cb_vt_hbm)[k // 2].at[0, 0, 0, :, pl.ds(k % 2 * wide, wide)]

    loads = [
        pltpu.make_async_copy(src, dst, in_sem.at[k])
        for k, (src, dst) in enumerate(
            [
                (pivot_hbm, pivot),
                (col_rank_hbm, col_rank),
                (row_rank_hbm, row_rank),
                (cb_rank_hbm, cb_rank),
                (pmap_hbm, pmap),
                (col_ut_hbm, col_ut),
                (col_vt_hbm, col_vt),
                (row_ut_hbm, row_ut),
                (row_vt_hbm, row_vt),
            ]
            + [(chunk_src(k), cbuf[k].at[r]) for k in range(4)]
        )
    ]
    for load in loads:
        load.start()

    barrier = pltpu.get_barrier_semaphore()

    def greet(target):
        pl.semaphore_signal(barrier, inc=1, device_id=target, device_id_type=MESH)

    greet((sibling, r, c))
    greet((front, r, partner))
    for p in peers:
        greet((front, r, p))

    @pl.when(has_left)
    def _():
        greet((front, r - 1, c))

    @pl.when(has_right)
    def _():
        greet((front, r + 1, c))

    for load in loads:
        load.wait()
    me = r * n_col + c
    rows_at = lax.broadcasted_iota(jnp.int32, (mr, tile), 0) + me * mr
    lanes_at = lax.broadcasted_iota(jnp.int32, (mr, tile), 1)
    on_diag = rows_at == lanes_at
    mine = pivot[0]
    inv = 1.0 / jnp.sum(jnp.where(on_diag, mine, 0.0), axis=1, keepdims=True)
    mbuf[me] = jnp.where(on_diag, inv, mine * inv).astype(BF16)

    def masked(value, rank):
        level = lax.broadcasted_iota(jnp.int32, value.shape, 0)
        return jnp.where(level < rank, value.astype(F32), 0.0).astype(BF16)

    fbuf[me] = jnp.concatenate(
        [
            col_ut[0, 0],
            masked(col_vt[0, 0], col_rank[0, 0]),
            masked(row_ut[0, 0], row_rank[0, 0]),
            row_vt[0, 0],
        ],
        axis=1,
    )
    for k in range(2):
        cbuf[k][r] = masked(cbuf[k][r], cb_rank[0, 0, 0])

    greeted = 2 + len(peers) + has_left.astype(jnp.int32) + has_right.astype(jnp.int32)
    pl.semaphore_wait(barrier, greeted)

    def copy(ref, send, recv, target):
        return pltpu.make_async_remote_copy(
            src_ref=ref, dst_ref=ref, send_sem=send, recv_sem=recv, device_id=target, device_id_type=MESH
        )

    left_dev, right_dev = (front, r - 1, c), (front, r + 1, c)
    partner_dev = (front, r, partner)
    panel = (fbuf, mbuf)

    def pcopy(t, q, cc, k, target):
        slot = q * n_col + cc
        return copy(panel[t].at[slot], ssem_p.at[t, slot, k], rsem_p.at[t, slot], target)

    def zcopy(t, q, k, target):
        if t < 2:
            return pcopy(t, q, c, k, target)
        return copy(cbuf[t - 2].at[q], ssem_c.at[t - 2, q, k], rsem_c.at[t - 2, q], target)

    def z_start(t, q, to_right, to_left):
        if to_right:

            @pl.when(has_right)
            def _():
                zcopy(t, q, 2, right_dev).start()

        if to_left:

            @pl.when(has_left)
            def _():
                zcopy(t, q, 1, left_dev).start()

        if t < 2:
            for k, p in enumerate(peers):
                pcopy(t, q, c, 3 + k, (front, r, p)).start()
            pcopy(t, q, c, 0, partner_dev).start()

    def z_own(t):
        z_start(t, r, True, True)

    def z_rest(t):
        for s in range(1, n_row):

            @pl.when(r - s >= 0)
            def _():
                zcopy(t, r - s, 0, partner_dev).wait_recv()
                z_start(t, r - s, True, False)

            @pl.when(r + s < n_row)
            def _():
                zcopy(t, r + s, 0, partner_dev).wait_recv()
                z_start(t, r + s, False, True)

    others = [lax.rem(x + k, n_x) * 2 + 1 - core for k in range(n_x)]

    def panel_relay(t):
        for s in range(n_row):

            def relay(q):
                for p in peers:
                    pcopy(t, q, p, 0, partner_dev).wait_recv()
                    pcopy(t, q, p, 0, partner_dev).start()

            @pl.when(r - s >= 0)
            def _():
                relay(r - s)

            if s > 0:

                @pl.when(r + s < n_row)
                def _():
                    relay(r + s)

    def find(wanted):
        at, found = jnp.int32(0), jnp.int32(0)
        for i in range(pmap.shape[1]):
            hit = pmap[0, i] == wanted
            at, found = jnp.where(hit, i, at), jnp.where(hit, 1, found)
        return at, found.astype(F32)

    i_at = [find(2 * r + u) for u in range(2)]
    j_own, j_sib = find(2 * c + half), find(2 * c + 1 - half)

    def kept(value, flag):
        return (value.astype(F32) * flag).astype(BF16)

    def scopy(k, cc, lane, target):
        return copy(sbuf[k].at[cc], ssem_s.at[k, cc, lane], rsem_s.at[k, cc], target)

    def share(k):
        for u in range(2):
            at, found = i_at[u]
            value = cbuf[k][at]
            sbuf[k][c, u] = kept(value, found) if k < 2 else value
        for lane, p in enumerate(peers):
            scopy(k, c, 1 + lane, (front, r, p)).start()
        scopy(k, c, 0, partner_dev).start()

    def share_relay(k):
        for p in peers:
            scopy(k, p, 0, partner_dev).wait_recv()
            scopy(k, p, 0, partner_dev).start()

    ends = [(ybuf.at[k], zbuf.at[k]) for k in range(4)] + [(yr, zr), (yd, zd)]

    def ycopy(t):
        return pltpu.make_async_remote_copy(
            src_ref=ends[t][0],
            dst_ref=ends[t][1],
            send_sem=ssem_y.at[t],
            recv_sem=rsem_y.at[t],
            device_id=(sibling, r, c),
            device_id_type=MESH,
        )

    def across(k):
        for p in others:
            scopy(k, p, 0, partner_dev).wait_recv()
        for u in range(2):
            value = sbuf[k][j_sib[0], u]
            ybuf[k, u] = kept(value, j_sib[1]) if k < 2 else value
        ycopy(k).start()

    for t in range(3):
        z_own(t)
    z_rest(0)
    z_own(3)
    z_rest(1)
    z_own(4)
    z_rest(2)
    z_own(5)
    share(0)
    panel_relay(0)
    panel_relay(1)
    z_rest(3)
    share(1)
    for t in range(2):
        for q in range(n_row):
            for p in others:
                pcopy(t, q, p, 0, partner_dev).wait_recv()

    pivots = mbuf[...].reshape(tile, tile)
    diag_blocks = []
    lane_block = 128
    for b in range(tile // lane_block):
        total = jnp.zeros((1, lane_block), F32)
        for d in range(lane_block // mr):
            dev = b * (lane_block // mr) + d
            piece = mbuf[dev, :, b * lane_block : (b + 1) * lane_block].astype(F32)
            at_r = lax.broadcasted_iota(jnp.int32, piece.shape, 0) + d * mr
            at_l = lax.broadcasted_iota(jnp.int32, piece.shape, 1)
            total = total + jnp.sum(jnp.where(at_r == at_l, piece, 0.0), axis=0, keepdims=True)
        diag_blocks.append(total)
    diag = jnp.concatenate(diag_blocks, axis=1)

    def col_piece(at, first):
        return jnp.concatenate(
            [fbuf[at * n_col + k][:, first : first + wc] for k in range(n_col)], axis=1
        )

    def row_piece(at, first):
        return jnp.concatenate(
            [fbuf[k * n_col + at][:, first : first + wr] for k in range(n_row)], axis=1
        )

    v = jnp.concatenate([col_piece(i_at[u][0], wc) for u in range(2)], axis=0)
    v32 = v.astype(F32)
    t = v
    for step in range(3):
        t32 = v32 - (mm(t, pivots, ((1,), (0,))) - t.astype(F32) * diag)
        t = t32.astype(BF16)
    lower = (t32 * diag).astype(BF16)
    col_u = [col_piece(i_at[u][0], 0) for u in range(2)]

    def updates(j):
        at, found = j
        core_ = mm(lower, row_piece(at, 2 * wc), ((1,), (1,))).astype(BF16)
        return [
            (
                mm(core_[u * rank_dim : (u + 1) * rank_dim], col_u[u], ((0,), (0,)))
                * (-found * i_at[u][1])
            ).astype(BF16)
            for u in range(2)
        ]

    yr[...] = row_piece(j_sib[0], 2 * wc + wr)
    ycopy(4).start()
    for u, value in enumerate(updates(j_sib)):
        yd[u] = value
    ycopy(5).start()

    share_relay(0)
    z_rest(4)
    share(2)
    share_relay(1)
    across(0)
    z_rest(5)
    share(3)
    share_relay(2)
    across(1)
    own = updates(j_own)
    own_r = row_piece(j_own[0], 2 * wc + wr)
    share_relay(3)
    across(2)
    across(3)

    ycopy(4).wait_recv()
    ycopy(5).wait_recv()
    for k in range(2):
        ycopy(k).wait_recv()
    lefts = []
    for u in range(2):
        from_cb = [
            jnp.concatenate([kept(sbuf[k][j_own[0], u], j_own[1]) for k in range(2)], axis=1),
            jnp.concatenate([zbuf[k, u] for k in range(2)], axis=1),
        ]
        lefts.append(jnp.concatenate([from_cb[0], own[u], from_cb[1], zd[u]], axis=0))
    for k in range(2):
        ycopy(2 + k).wait_recv()
        lanes = slice(k * wide, (k + 1) * wide)
        for u in range(2):
            right = jnp.concatenate(
                [sbuf[2 + k][j_own[0], u], own_r[:, lanes], zbuf[2 + k, u], zr[:, lanes]], axis=0
            )
            out[0, u, 0, :, lanes] = mm(lefts[u], right, ((0,), (0,))).astype(BF16)

    for t in range(6):
        ycopy(t).wait_send()
    for k in range(4):
        for lane, p in enumerate(peers):
            scopy(k, c, 1 + lane, partner_dev).wait_send()
            scopy(k, p, 0, partner_dev).wait_send()
        scopy(k, c, 0, partner_dev).wait_send()
    for q in range(n_row):
        for t in range(2):
            for k, p in enumerate(peers):
                pcopy(t, q, c, 3 + k, partner_dev).wait_send()
                pcopy(t, q, p, 0, partner_dev).wait_send()
            pcopy(t, q, c, 0, partner_dev).wait_send()

        @pl.when((q <= r) & has_right)
        def _():
            for t in range(6):
                zcopy(t, q, 2, partner_dev).wait_send()

        @pl.when((q >= r) & has_left)
        def _():
            for t in range(6):
                zcopy(t, q, 1, partner_dev).wait_send()


def shards(
    n_row,
    n_col,
    pivot,
    col_ut,
    col_vt,
    col_rank,
    row_ut,
    row_vt,
    row_rank,
    cb_ut,
    cb_vt,
    cb_rank,
    parent_map,
):
    n_x = n_col // 2
    mr = pivot.shape[1]
    rank_dim, tile = cb_ut.shape[-2], cb_ut.shape[-1]
    width = 2 * col_ut.shape[-1] + 2 * row_ut.shape[-1]
    vmem = pl.BlockSpec(memory_space=pltpu.VMEM)
    hbm = pl.BlockSpec(memory_space=pltpu.HBM)
    pair = (2, rank_dim, tile)
    half = (rank_dim, tile // 2)
    dma = pltpu.SemaphoreType.DMA
    return pl.pallas_call(
        functools.partial(kernel, n_row, n_col),
        out_shape=jax.ShapeDtypeStruct((1, 2, 1, tile, tile), BF16),
        in_specs=[hbm] * 11,
        out_specs=vmem,
        scratch_shapes=[
            pltpu.VMEM(pivot.shape, F32),
            pltpu.VMEM(col_ut.shape, BF16),
            pltpu.VMEM(col_vt.shape, BF16),
            pltpu.VMEM(row_ut.shape, BF16),
            pltpu.VMEM(row_vt.shape, BF16),
            pltpu.SMEM(col_rank.shape, jnp.int32),
            pltpu.SMEM(row_rank.shape, jnp.int32),
            pltpu.SMEM(cb_rank.shape, jnp.int32),
            pltpu.SMEM(parent_map.shape, jnp.int32),
            pltpu.VMEM((n_row * n_col, mr, tile), BF16),
            pltpu.VMEM((n_row * n_col, rank_dim, width), BF16),
            *[pltpu.VMEM((n_row,) + half, BF16)] * 4,
            *[pltpu.VMEM((n_col, 2) + half, BF16)] * 4,
            pltpu.VMEM((4, 2) + half, BF16),
            pltpu.VMEM(pair, BF16),
            pltpu.VMEM(pair[1:], BF16),
            pltpu.VMEM((4, 2) + half, BF16),
            pltpu.VMEM(pair, BF16),
            pltpu.VMEM(pair[1:], BF16),
            dma((13,)),
            dma((2, n_row * n_col)),
            dma((2, n_row * n_col, 2 + n_x)),
            dma((4, n_row)),
            dma((4, n_row, 3)),
            dma((4, n_col)),
            dma((4, n_col, n_x)),
            dma((6,)),
            dma((6,)),
        ],
        compiler_params=pltpu.CompilerParams(
            collective_id=0, has_side_effects=True, vmem_limit_bytes=67043328
        ),
    )(
        pivot,
        col_ut,
        col_vt,
        row_ut,
        row_vt,
        cb_ut,
        cb_vt,
        col_rank,
        row_rank,
        cb_rank,
        parent_map,
    )


def solution(mesh):
    placed = (
        P("front", ("row", "col"), None),
        P("front", "row", None, "col"),
        P("front", "row", None, "col"),
        P("front", "row"),
        P("front", "col", None, "row"),
        P("front", "col", None, "row"),
        P("front", "col"),
        P("front", "row", "col", None, None),
        P("front", "row", "col", None, None),
        P("front", "row", "col"),
        P("front", None),
    )
    return jax.shard_map(
        functools.partial(shards, mesh.shape["row"], mesh.shape["col"]),
        mesh=mesh,
        in_specs=placed,
        out_specs=P("front", "row", "col", None, None),
        check_vma=False,
    )
```

time: 59.7 us -> 53.9 us (0.903)
  local copies, waits for them, and re-layouts: 6.54 us -> 2.26 us
  Pallas kernels: 50.6 us -> 49.4 us
    unnamed x17 -> x1, local copies, waits for them, and re-layouts: 6.54 us -> 2.26 us
    pallas_call x1, Pallas kernels: 50.6 us -> 49.4 us  [shards(): pl.pallas_call(functools.partial(kernel, n_row, n_col), out_shape=jax.Sha...]
where the time goes in v2:
time: 53.9 us; the launch traced here: 53.6 us
  Pallas kernels  49.4 us (92%)
  local copies, waits for them, and re-layouts  2.26 us (4%)
  between operations  1.95 us (4%)
    pallas_call x1, Pallas kernels, shards(): pl.pallas_call(functools.partial(kernel, n_row, n_col), out_shape=jax.Sha...  49.4 us
    unnamed x1, local copies, waits for them, and re-layouts  2.26 us

profile of v2, /device:TPU:0, one launch (start us, length us, event | category | flops | bytes accessed | tf_op | source)
XLA Modules:
  0.0 53.6 jit_solution(7041344863750925724)
XLA Ops:
  1.9 49.4 %shard_map.109 = bf16[1,2,1,512,512]{4,3,2,1,0:T(8,128)(2,1)} custom-call(f32[1,32,512]{2,1,0:T(8,128)} %pivot_hbm.1, bf16[1,1,96,128]{3,2,1,0:T(8,128)(2,1)} %col_ut_hbm.1, bf16[1,1,96,128]{3,2,1,0:T(8,128)(2,1)} %col_vt_hbm.1, bf16[1,1,96,128]{3,2,1,0:T(8,128)(2,1)} %row_ut_hbm.1, bf16[1,1,96,128]{3,2,1,0:T(8,128)(2,1)} %row_vt_hbm.1, ...), custom_call_target="tpu_custom_call" | custom-call | tf_op jit(solution)/shard_map/pallas_call | solution.py:427
  51.4 2.3 %copy.16 = bf16[1,2,1,512,512]{4,3,2,1,0:T(8,128)(2,1)} copy(bf16[1,2,1,512,512]{4,3,2,1,0:T(8,128)(2,1)} %shard_map.109) | data formatting | bytes 2097152

commit v3 on v2

--- a/solution.py
+++ b/solution.py
@@ -189,38 +189,34 @@
     def z_own(t):
         z_start(t, r, True, True)
 
-    def z_rest(t):
-        for s in range(1, n_row):
-
-            @pl.when(r - s >= 0)
-            def _():
-                zcopy(t, r - s, 0, partner_dev).wait_recv()
-                z_start(t, r - s, True, False)
+    def z_hop(t, s):
+        @pl.when(r - s >= 0)
+        def _():
+            zcopy(t, r - s, 0, partner_dev).wait_recv()
+            z_start(t, r - s, True, False)
+
+        @pl.when(r + s < n_row)
+        def _():
+            zcopy(t, r + s, 0, partner_dev).wait_recv()
+            z_start(t, r + s, False, True)
+
+    others = [lax.rem(x + k, n_x) * 2 + 1 - core for k in range(n_x)]
+
+    def panel_relay(t, s):
+        def relay(q):
+            for p in peers:
+                pcopy(t, q, p, 0, partner_dev).wait_recv()
+                pcopy(t, q, p, 0, partner_dev).start()
+
+        @pl.when(r - s >= 0)
+        def _():
+            relay(r - s)
+
+        if s > 0:
 
             @pl.when(r + s < n_row)
             def _():
-                zcopy(t, r + s, 0, partner_dev).wait_recv()
-                z_start(t, r + s, False, True)
-
-    others = [lax.rem(x + k, n_x) * 2 + 1 - core for k in range(n_x)]
-
-    def panel_relay(t):
-        for s in range(n_row):
-
-            def relay(q):
-                for p in peers:
-                    pcopy(t, q, p, 0, partner_dev).wait_recv()
-                    pcopy(t, q, p, 0, partner_dev).start()
-
-            @pl.when(r - s >= 0)
-            def _():
-                relay(r - s)
-
-            if s > 0:
-
-                @pl.when(r + s < n_row)
-                def _():
-                    relay(r + s)
+                relay(r + s)
 
     def find(wanted):
         at, found = jnp.int32(0), jnp.int32(0)
@@ -272,38 +268,6 @@
             ybuf[k, u] = kept(value, j_sib[1]) if k < 2 else value
         ycopy(k).start()
 
-    for t in range(3):
-        z_own(t)
-    z_rest(0)
-    z_own(3)
-    z_rest(1)
-    z_own(4)
-    z_rest(2)
-    z_own(5)
-    share(0)
-    panel_relay(0)
-    panel_relay(1)
-    z_rest(3)
-    share(1)
-    for t in range(2):
-        for q in range(n_row):
-            for p in others:
-                pcopy(t, q, p, 0, partner_dev).wait_recv()
-
-    pivots = mbuf[...].reshape(tile, tile)
-    diag_blocks = []
-    lane_block = 128
-    for b in range(tile // lane_block):
-        total = jnp.zeros((1, lane_block), F32)
-        for d in range(lane_block // mr):
-            dev = b * (lane_block // mr) + d
-            piece = mbuf[dev, :, b * lane_block : (b + 1) * lane_block].astype(F32)
-            at_r = lax.broadcasted_iota(jnp.int32, piece.shape, 0) + d * mr
-            at_l = lax.broadcasted_iota(jnp.int32, piece.shape, 1)
-            total = total + jnp.sum(jnp.where(at_r == at_l, piece, 0.0), axis=0, keepdims=True)
-        diag_blocks.append(total)
-    diag = jnp.concatenate(diag_blocks, axis=1)
-
     def col_piece(at, first):
         return jnp.concatenate(
             [fbuf[at * n_col + k][:, first : first + wc] for k in range(n_col)], axis=1
@@ -314,16 +278,7 @@
             [fbuf[k * n_col + at][:, first : first + wr] for k in range(n_row)], axis=1
         )
 
-    v = jnp.concatenate([col_piece(i_at[u][0], wc) for u in range(2)], axis=0)
-    v32 = v.astype(F32)
-    t = v
-    for step in range(3):
-        t32 = v32 - (mm(t, pivots, ((1,), (0,))) - t.astype(F32) * diag)
-        t = t32.astype(BF16)
-    lower = (t32 * diag).astype(BF16)
-    col_u = [col_piece(i_at[u][0], 0) for u in range(2)]
-
-    def updates(j):
+    def updates(lower, col_u, j):
         at, found = j
         core_ = mm(lower, row_piece(at, 2 * wc), ((1,), (1,))).astype(BF16)
         return [
@@ -334,26 +289,59 @@
             for u in range(2)
         ]
 
-    yr[...] = row_piece(j_sib[0], 2 * wc + wr)
-    ycopy(4).start()
-    for u, value in enumerate(updates(j_sib)):
-        yd[u] = value
-    ycopy(5).start()
-
-    share_relay(0)
-    z_rest(4)
-    share(2)
-    share_relay(1)
-    across(0)
-    z_rest(5)
-    share(3)
-    share_relay(2)
-    across(1)
-    own = updates(j_own)
-    own_r = row_piece(j_own[0], 2 * wc + wr)
-    share_relay(3)
-    across(2)
-    across(3)
+    def pivoting():
+        for t in range(2):
+            for q in range(n_row):
+                for p in others:
+                    pcopy(t, q, p, 0, partner_dev).wait_recv()
+        yr[...] = row_piece(j_sib[0], 2 * wc + wr)
+        ycopy(4).start()
+        pivots = mbuf[...].reshape(tile, tile)
+        diag_blocks = []
+        lane_block = 128
+        for b in range(tile // lane_block):
+            total = jnp.zeros((1, lane_block), F32)
+            for d in range(lane_block // mr):
+                dev = b * (lane_block // mr) + d
+                piece = mbuf[dev, :, b * lane_block : (b + 1) * lane_block].astype(F32)
+                at_r = lax.broadcasted_iota(jnp.int32, piece.shape, 0) + d * mr
+                at_l = lax.broadcasted_iota(jnp.int32, piece.shape, 1)
+                total = total + jnp.sum(jnp.where(at_r == at_l, piece, 0.0), axis=0, keepdims=True)
+            diag_blocks.append(total)
+        diag = jnp.concatenate(diag_blocks, axis=1)
+        v = jnp.concatenate([col_piece(i_at[u][0], wc) for u in range(2)], axis=0)
+        v32 = v.astype(F32)
+        t = v
+        for step in range(3):
+            t32 = v32 - (mm(t, pivots, ((1,), (0,))) - t.astype(F32) * diag)
+            t = t32.astype(BF16)
+        lower = (t32 * diag).astype(BF16)
+        col_u = [col_piece(i_at[u][0], 0) for u in range(2)]
+        for u, value in enumerate(updates(lower, col_u, j_sib)):
+            yd[u] = value
+        ycopy(5).start()
+        return updates(lower, col_u, j_own), row_piece(j_own[0], 2 * wc + wr)
+
+    last, ahead = n_row - 1, 3
+    for t in range(ahead + 1):
+        z_own(t)
+    for d in range(1, last + 9):
+        if ahead + d < 6:
+            z_own(ahead + d)
+        for s in range(last, 0, -1):
+            if 0 <= d - s < 6:
+                z_hop(d - s, s)
+        if 0 <= d - last - 2 < 4:
+            share(d - last - 2)
+        for t in range(2):
+            if 0 <= d - t - 1 <= last:
+                panel_relay(t, d - t - 1)
+        if d == last + 3:
+            own, own_r = pivoting()
+        if 0 <= d - last - 4 < 4:
+            share_relay(d - last - 4)
+        if 0 <= d - last - 5 < 4:
+            across(d - last - 5)
 
     ycopy(4).wait_recv()
     ycopy(5).wait_recv()

time: 53.9 us -> 52 us (0.965)
  Pallas kernels: 49.4 us -> 47.5 us
    pallas_call x1, Pallas kernels: 49.4 us -> 47.5 us  [shards(): pl.pallas_call(functools.partial(kernel, n_row, n_col), out_shape=jax.Sha...]
where the time goes in v3:
time: 52 us; the launch traced here: 51.7 us
  Pallas kernels  47.5 us (91%)
  local copies, waits for them, and re-layouts  2.26 us (4%)
  between operations  1.95 us (4%)
    pallas_call x1, Pallas kernels, shards(): pl.pallas_call(functools.partial(kernel, n_row, n_col), out_shape=jax.Sha...  47.5 us
    unnamed x1, local copies, waits for them, and re-layouts  2.26 us

profile of v3, /device:TPU:0, one launch (start us, length us, event | category | flops | bytes accessed | tf_op | source)
XLA Modules:
  0.0 51.7 jit_solution(2963583642934322420)
XLA Ops:
  1.9 47.5 %shard_map.109 = bf16[1,2,1,512,512]{4,3,2,1,0:T(8,128)(2,1)} custom-call(f32[1,32,512]{2,1,0:T(8,128)} %pivot_hbm.1, bf16[1,1,96,128]{3,2,1,0:T(8,128)(2,1)} %col_ut_hbm.1, bf16[1,1,96,128]{3,2,1,0:T(8,128)(2,1)} %col_vt_hbm.1, bf16[1,1,96,128]{3,2,1,0:T(8,128)(2,1)} %row_ut_hbm.1, bf16[1,1,96,128]{3,2,1,0:T(8,128)(2,1)} %row_vt_hbm.1, ...), custom_call_target="tpu_custom_call" | custom-call | tf_op jit(solution)/shard_map/pallas_call | solution.py:415
  49.5 2.3 %copy.16 = bf16[1,2,1,512,512]{4,3,2,1,0:T(8,128)(2,1)} copy(bf16[1,2,1,512,512]{4,3,2,1,0:T(8,128)(2,1)} %shard_map.109) | data formatting | bytes 2097152

commit v4 on v3

--- a/solution.py
+++ b/solution.py
@@ -322,26 +322,26 @@
         ycopy(5).start()
         return updates(lower, col_u, j_own), row_piece(j_own[0], 2 * wc + wr)
 
-    last, ahead = n_row - 1, 3
-    for t in range(ahead + 1):
+    last, lag = n_row - 1, 3
+    for t in range(6):
         z_own(t)
-    for d in range(1, last + 9):
-        if ahead + d < 6:
-            z_own(ahead + d)
+    for d in range(lag * last + 11):
         for s in range(last, 0, -1):
-            if 0 <= d - s < 6:
-                z_hop(d - s, s)
-        if 0 <= d - last - 2 < 4:
-            share(d - last - 2)
+            if 0 <= d - lag * s < 6:
+                z_hop(d - lag * s, s)
+        k = d - lag * last - 2
+        if 0 <= k < 4:
+            share(k)
         for t in range(2):
-            if 0 <= d - t - 1 <= last:
-                panel_relay(t, d - t - 1)
-        if d == last + 3:
+            for s in range(n_row):
+                if d - t - 2 == lag * s:
+                    panel_relay(t, s)
+        if k == 2:
             own, own_r = pivoting()
-        if 0 <= d - last - 4 < 4:
-            share_relay(d - last - 4)
-        if 0 <= d - last - 5 < 4:
-            across(d - last - 5)
+        if 0 <= k - 3 < 4:
+            share_relay(k - 3)
+        if 0 <= k - 5 < 4:
+            across(k - 5)
 
     ycopy(4).wait_recv()
     ycopy(5).wait_recv()

time: 52 us -> 52.4 us (level)
  no operation moved by 1% of the time
where the time goes in v4:
time: 52.4 us; the launch traced here: 52.2 us
  Pallas kernels  48 us (92%)
  local copies, waits for them, and re-layouts  2.26 us (4%)
  between operations  1.95 us (4%)
    pallas_call x1, Pallas kernels, shards(): pl.pallas_call(functools.partial(kernel, n_row, n_col), out_shape=jax.Sha...  48 us
    unnamed x1, local copies, waits for them, and re-layouts  2.26 us

profile of v4, /device:TPU:0, one launch (start us, length us, event | category | flops | bytes accessed | tf_op | source)
XLA Modules:
  0.0 52.2 jit_solution(17444051521283634304)
XLA Ops:
  1.9 48.0 %shard_map.109 = bf16[1,2,1,512,512]{4,3,2,1,0:T(8,128)(2,1)} custom-call(f32[1,32,512]{2,1,0:T(8,128)} %pivot_hbm.1, bf16[1,1,96,128]{3,2,1,0:T(8,128)(2,1)} %col_ut_hbm.1, bf16[1,1,96,128]{3,2,1,0:T(8,128)(2,1)} %col_vt_hbm.1, bf16[1,1,96,128]{3,2,1,0:T(8,128)(2,1)} %row_ut_hbm.1, bf16[1,1,96,128]{3,2,1,0:T(8,128)(2,1)} %row_vt_hbm.1, ...), custom_call_target="tpu_custom_call" | custom-call | tf_op jit(solution)/shard_map/pallas_call | solution.py:415
  49.9 2.3 %copy.16 = bf16[1,2,1,512,512]{4,3,2,1,0:T(8,128)(2,1)} copy(bf16[1,2,1,512,512]{4,3,2,1,0:T(8,128)(2,1)} %shard_map.109) | data formatting | bytes 2097152
